TPU v7x, 256 devices: a whole 4x4x8 slice. The times are simulated.
256 devices in a mesh: dp: 32 (over z, x), mp: 4 (over y), mc: 2 (over core).
Axes of the slice: x: 4, y: 4, z: 8, core: 2. Of those that a mesh axis runs over, the one named last changes fastest.
Arguments:
- features: bfloat16 [12608, 768], P('dp'), may hold values from -6 to 6
- out_cotangent: bfloat16 [2, 12608, 768], P('mc', 'dp'), may hold values from -6 to 6
- mean_up: float32 [768, 3072], P('dp', 'mp'), may hold values from -0.21875 to 0.21875
- precision_up: float32 [768, 3072], P('dp', 'mp'), may hold values from 4 to 64
- noise_up: float32 [2, 768, 3072], P('mc', 'dp', 'mp'), may hold values from -6 to 6
- mean_down: float32 [768, 3072], P('dp', 'mp'), may hold values from -0.109375 to 0.109375
- precision_down: float32 [768, 3072], P('dp', 'mp'), may hold values from 4 to 64
- noise_down: float32 [2, 768, 3072], P('mc', 'dp', 'mp'), may hold values from -6 to 6
Outputs:
- mean_new_up: float32 [768, 3072], P('dp', 'mp')
- precision_new_up: float32 [768, 3072], P('dp', 'mp')
- mean_new_down: float32 [768, 3072], P('dp', 'mp')
- precision_new_down: float32 [768, 3072], P('dp', 'mp')
- input_grad: bfloat16 [2, 12608, 768], P('mc', 'dp', 'mp')
All inputs are finite; a program needn't handle non-finite values.
Results may differ from a plain program's by a relative error of at most 0.0015.
The roundings to bfloat16 on the way count: a program that leaves them out, or rounds other values in their place, can miss the bound.
Values may be sent and summed in bfloat16 or wider, within the bound.
No kernel may reach another device: no remote copies, remote signals or barrier semaphores. Data moves between devices by JAX's collectives and lax.ppermute only.
A program may use at most 64 MiB of HBM per device.

v0:
```python
import jax
import jax.numpy as jnp
from jax import lax
from jax.sharding import Mesh
from jax.sharding import PartitionSpec as P

D = 768
FF = 3072
PATCHES = 197
DP = ("dp_0", "dp_1")
DP_MC = ("dp_0", "dp_1", "mc")
DP_MP = ("dp_0", "dp_1", "mp")
reciprocal_root = 0.7071067811865476
normal_peak = 0.3989422804014327
tempering = 100.0
damping = 4.0
average_rate = 0.25
step_rate = 0.05
clip_level = 0.01


def sent_together(arrays, axis, dim, along):
    widths = [a.shape[along] for a in arrays]
    both = jnp.concatenate(arrays, axis=along)
    filled = lax.all_gather(both, axis, axis=dim, tiled=True)
    return tuple(jnp.split(filled, [sum(widths[:k]) for k in range(1, len(widths))], axis=along))


def split_up(value, dim, devices):
    shape = value.shape
    tiles = value.reshape(*shape[:dim], devices, shape[dim] // devices, *shape[dim + 1 :])
    return jnp.moveaxis(tiles, dim, 0)


def sum_at_owner(value, axis, dim):
    devices = lax.axis_size(axis)
    tiles = lax.all_to_all(split_up(value, dim, devices), axis, 0, 0, tiled=True)
    return jnp.sum(tiles, axis=0)


def sum_together(arrays, axis, dims):
    devices = lax.axis_size(axis)
    tiles = [split_up(a, dim, devices) for a, dim in zip(arrays, dims)]
    lines = jnp.concatenate([b.reshape(devices, -1) for b in tiles], axis=1)
    span = max(16, -(-lines.shape[1] // 1024) * 8)
    lines = jnp.pad(lines, ((0, 0), (0, span * 128 - lines.shape[1]))).reshape(-1, 128)
    line, at, gathered = (lax.psum_scatter(lines, axis, tiled=True).reshape(-1), 0, [])
    for b in tiles:
        part = b[0]
        gathered.append(line[at : at + part.size].reshape(part.shape))
        at += part.size
    return tuple(gathered)


def one_axis_at_a_time(value, axes):
    for axis in axes:
        value = lax.psum(value, axis)
    return value


def gelu_parts(preact):
    cumulative = 0.5 * (1.0 + lax.erf(preact * reciprocal_root))
    density = normal_peak * jnp.exp(-0.5 * preact * preact)
    return (preact * cumulative, cumulative + preact * density)


def sample_weights(center, precision, noise_draw):
    spread = 1.0 / jnp.sqrt(tempering * (precision + damping))
    return (center + spread * noise_draw).astype(jnp.bfloat16)


def contract_rows(left, right):
    return lax.dot_general(
        left, right, (((0,), (0,)), ((), ())), preferred_element_type=jnp.float32
    )


def contract_cols(left, right):
    return lax.dot_general(
        left, right, (((1,), (1,)), ((), ())), preferred_element_type=jnp.float32
    )


def shards(
    features, out_cotangent, mean_up, precision_up, noise_up, mean_down, precision_down, noise_down
):
    shard_up = sample_weights(mean_up, precision_up, noise_up[0])
    shard_down = sample_weights(mean_down, precision_down, noise_down[0])
    w_up, w_down = sent_together((shard_up, shard_down), DP, 0, 1)
    cotangent = out_cotangent[0]
    preact = jnp.dot(features, w_up, preferred_element_type=jnp.float32)
    gelu_value, gelu_slope = gelu_parts(preact)
    hidden = gelu_value.astype(jnp.bfloat16)
    hidden_grad = jnp.dot(cotangent, w_down, preferred_element_type=jnp.float32)
    preact_grad = (hidden_grad * gelu_slope).astype(jnp.bfloat16)
    partial_value = contract_cols(preact_grad, w_up)
    input_grad = sum_at_owner(partial_value, "mp", 1).astype(jnp.bfloat16)[None]
    images = features.shape[0] // PATCHES
    empty_sum = jnp.zeros(w_up.shape, jnp.float32)

    def accumulate(image_index, totals):
        offset = image_index * PATCHES
        image_rows = lax.dynamic_slice_in_dim(features, offset, PATCHES, 0)
        cotangent_rows = lax.dynamic_slice_in_dim(cotangent, offset, PATCHES, 0)
        grad_rows = lax.dynamic_slice_in_dim(preact_grad, offset, PATCHES, 0)
        hidden_rows = lax.dynamic_slice_in_dim(hidden, offset, PATCHES, 0)
        grad_up = contract_rows(image_rows, grad_rows)
        grad_down = contract_rows(cotangent_rows, hidden_rows)
        return (
            totals[0] + grad_up,
            totals[1] + grad_up * grad_up,
            totals[2] + grad_down,
            totals[3] + grad_down * grad_down,
        )

    totals = lax.fori_loop(0, images, accumulate, (empty_sum, empty_sum, empty_sum, empty_sum))
    shares = sum_together((totals[0], totals[1], totals[2], totals[3]), DP_MC, (0, 0, 0, 0))
    reduced = sent_together((shares[0], shares[1], shares[2], shares[3]), "mc", 0, 1)
    samples = lax.axis_size("mc")
    images_all = images * lax.axis_size(DP)
    grad_up = reduced[0] / samples
    square_up = reduced[1] / (samples * images_all)
    grad_down = reduced[2] / samples
    square_down = reduced[3] / (samples * images_all)
    precision_new_up = (1.0 - average_rate) * precision_up + average_rate * square_up
    precision_new_down = (1.0 - average_rate) * precision_down + average_rate * square_down
    raw_up = grad_up / (precision_new_up + damping)
    raw_down = grad_down / (precision_new_down + damping)
    local_sum = jnp.sum(raw_up * raw_up) + jnp.sum(raw_down * raw_down)
    global_sum = one_axis_at_a_time(local_sum, DP_MP)
    root_mean = jnp.sqrt(global_sum / (2 * D * FF))
    factor = 1.0 / jnp.maximum(clip_level, root_mean)
    mean_new_up = mean_up - step_rate * factor * raw_up
    mean_new_down = mean_down - step_rate * factor * raw_down
    return (mean_new_up, precision_new_up, mean_new_down, precision_new_down, input_grad)


def solution(mesh):
    split = Mesh(
        mesh.devices.reshape(8, 4, mesh.shape["mp"], mesh.shape["mc"]), ("dp_0", "dp_1", "mp", "mc")
    )
    placed = (
        P(DP, None),
        P("mc", DP, None),
        P(DP, "mp"),
        P(DP, "mp"),
        P("mc", DP, "mp"),
        P(DP, "mp"),
        P(DP, "mp"),
        P("mc", DP, "mp"),
    )
    return jax.shard_map(
        shards,
        mesh=split,
        in_specs=placed,
        out_specs=(P(DP, "mp"), P(DP, "mp"), P(DP, "mp"), P(DP, "mp"), P("mc", DP, "mp")),
        check_vma=False,
    )
```

profile of v0, /device:TPU:2, one launch (start us, length us, event | category | flops | bytes accessed | tf_op | source)
XLA Modules:
  0.0 343.7 jit_solution(2468761831354975796)
XLA Ops:
  9.1 81.9 %all-gather.3.cloned.1.call-done = bf16[768,1536]{1,0:T(8,128)(2,1)} async-done(((bf16[24,1536]{1,0:T(8,128)(2,1)}), bf16[768,1536]{1,0:T(8,128)(2,1)}) %all-gather.3.cloned.1.call-update) | async-done | bytes 2359312 | tf_op jit(solution)/shard_map/all_gather | solution.py:25
  90.9 3.1 multiply_convert_fusion
  94.1 2.0 fusion.9
  96.1 15.9 %while.20 = (s32[]{:T(128)}, f32[768,768]{1,0:T(8,128)}, f32[768,768]{1,0:T(8,128)}, f32[768,768]{1,0:T(8,128)}, f32[768,768]{1,0:T(8,128)S(1)}, /*index=5*/bf16...) while((s32[]{:T(128)}, f32[768,768]{1,0:T(8,128)}, ...), condition=%wide.region_1.0_spmd.clone, body=%wide.region_0.0_spmd.clone.sunk | while | flops 470679552 | bytes 60276036 | solution.py:116
  96.1 4.0 %select_add_fusion.7 = (f32[768,768]{1,0:T(8,128)S(1)}, f32[768,768]{1,0:T(8,128)}) fusion(f32[768,768]{1,0:T(8,128)S(1)} %get-tuple-element.317, pred[]{:T(512)S(6)} %compare.3, f32[768,768]{1,0:T(8,128)} %get-tuple-element.316, bf16[394,768]{1,0:T(8,128)(2,1)} %get-tuple-element.334, s32[]{:T(128)S(6)} %select_n.12, ...), kind=kOutput, calls=%fused_computation.clone.1 | convolution fusion | flops 235339776 | bytes 10053120 | tf_op jit(solution)/shard_map/while/body/eval_jaxpr/dot_general | solution.py:73
  101.5 1.5 copy-done.2
  103.7 4.7 %select_add_fusion.7 = (f32[768,768]{1,0:T(8,128)S(1)}, f32[768,768]{1,0:T(8,128)}) fusion(f32[768,768]{1,0:T(8,128)S(1)} %get-tuple-element.317, pred[]{:T(512)S(6)} %compare.3, f32[768,768]{1,0:T(8,128)} %get-tuple-element.316, bf16[394,768]{1,0:T(8,128)(2,1)} %get-tuple-element.334, s32[]{:T(128)S(6)} %select_n.12, ...), kind=kOutput, calls=%fused_computation.clone.1 | convolution fusion | flops 235339776 | bytes 10053120 | tf_op jit(solution)/shard_map/while/body/eval_jaxpr/dot_general | solution.py:73
  109.8 1.5 copy-done.2
  112.0 1.8 reshape_reshape.15
  113.8 3.1 reshape_reshape.12
  116.8 3.2 reshape_reshape.13
  120.1 1.8 reshape_reshape.14
  121.9 6.4 %pad_maximum_fusion = f32[64,36864]{1,0:T(8,128)} fusion(f32[64,9216]{1,0:T(8,128)} %reshape_reshape.15, f32[64,9216]{1,0:T(8,128)} %reshape_reshape.14, f32[64,9216]{1,0:T(8,128)} %reshape_reshape.13, f32[64,9216]{1,0:T(8,128)} %reshape_reshape.12), kind=kLoop, calls=%fused_computation.12 | loop fusion | flops 7077888 | bytes 18874368 | tf_op jit(solution)/shard_map/concatenate | solution.py:44
  128.3 10.0 %reshape.45 = f32[18432,128]{1,0:T(8,128)} reshape(f32[64,36864]{1,0:T(8,128)} %pad_maximum_fusion) | data formatting | bytes 18874368 | tf_op jit(solution)/shard_map/reshape | solution.py:46
  138.3 1.6 copy-done.7
  139.9 1.7 fusion.15
  141.7 2.4 reshape.50
  144.1 1.8 copy.13
  145.9 4.4 %all-to-all-start = ((f32[4,394,192]{1,2,0:T(8,128)}), f32[4,394,192]{1,2,0:T(8,128)S(1)}, u32[]{:S(2)}, u32[]{:S(2)}) async-start(f32[4,394,192]{1,2,0:T(8,128)} %copy.13), calls=%async_computation.1 | async-start | bytes 3145728 | tf_op jit(solution)/shard_map/all_to_all | solution.py:37
  150.3 141.4 %reduce-scatter.2.cloned.1.call-done = f32[288,128]{1,0:T(8,128)} async-done(((f32[18432,128]{1,0:T(8,128)}), f32[288,128]{1,0:T(8,128)}) %reduce-scatter.2.cloned.1.call-update) | async-done | bytes 147472 | tf_op jit(solution)/shard_map/reduce_scatter | solution.py:47
  292.6 2.2 all-gather
  297.0 16.1 %psum.21 = f32[]{:T(128)} all-reduce(f32[]{:T(128)S(6)} %add.109), channel_id=1, replica_groups=mesh['dp_0'=8,'dp_1'=4,'mp'=4,'mc'=2] {'dp_0'}, use_global_device_ids=true, to_apply=%region_5.6 | all-reduce | flops 1 | bytes 8 | tf_op jit(solution)/shard_map/psum | solution.py:57
  313.3 10.2 %psum.22 = f32[]{:T(128)} all-reduce(f32[]{:T(128)} %psum.21), channel_id=1, replica_groups=mesh['dp_0'=8,'dp_1'=4,'mp'=4,'mc'=2] {'dp_1'}, use_global_device_ids=true, to_apply=%region_6.7 | all-reduce | flops 1 | bytes 8 | tf_op jit(solution)/shard_map/psum | solution.py:57
  324.3 11.1 %psum.23 = f32[]{:T(128)} all-reduce(f32[]{:T(128)} %psum.22), channel_id=1, replica_groups=mesh['dp_0'=8,'dp_1'=4,'mp'=4,'mc'=2] {'mp'}, use_global_device_ids=true, to_apply=%region_7.8 | all-reduce | flops 1 | bytes 8 | tf_op jit(solution)/shard_map/psum | solution.py:57
  (60 shorter events, 9.5 us)
Async XLA Ops:
  7.2 83.8 %all-gather.3.cloned.1.call-start = ((), (), s32[]{:S(2)}) async-start(), calls=%async_computation.2 | async-start | bytes 2433024 | tf_op jit(solution)/shard_map/all_gather | solution.py:25
  9.0 282.7 %reduce-scatter.2.cloned.1.call-start = ((), (), s32[]{:S(2)}) async-start(), calls=%async_computation.3 | async-start | bytes 9584640 | tf_op jit(solution)/shard_map/reduce_scatter | solution.py:47
  90.9 3.1 copy-start.6
  96.1 4.0 %copy-start.1 = (f32[768,768]{1,0:T(8,128)S(1)}, f32[768,768]{1,0:T(8,128)}, u32[]{:S(2)}) copy-start(f32[768,768]{1,0:T(8,128)} %get-tuple-element.315) | copy-start | bytes 7077892 | tf_op jit(solution)/shard_map/while
  96.1 4.0 %copy-start.3 = (f32[768,768]{1,0:T(8,128)S(1)}, f32[768,768]{1,0:T(8,128)}, u32[]{:S(2)}) copy-start(f32[768,768]{1,0:T(8,128)} %get-tuple-element.314) | copy-start | bytes 7077892 | tf_op jit(solution)/shard_map/while
  96.1 4.0 %copy-start.5 = (bf16[394,768]{1,0:T(8,128)(2,1)S(1)}, bf16[394,768]{1,0:T(8,128)(2,1)}, u32[]{:S(2)}) copy-start(bf16[394,768]{1,0:T(8,128)(2,1)} %get-tuple-element.331) | copy-start | bytes 1815556 | tf_op jit(solution)/shard_map/while
  101.4 1.5 copy-start.2
  101.4 2.2 copy-start.4
  103.7 4.8 %copy-start.1 = (f32[768,768]{1,0:T(8,128)S(1)}, f32[768,768]{1,0:T(8,128)}, u32[]{:S(2)}) copy-start(f32[768,768]{1,0:T(8,128)} %get-tuple-element.315) | copy-start | bytes 7077892 | tf_op jit(solution)/shard_map/while
  103.7 4.8 %copy-start.3 = (f32[768,768]{1,0:T(8,128)S(1)}, f32[768,768]{1,0:T(8,128)}, u32[]{:S(2)}) copy-start(f32[768,768]{1,0:T(8,128)} %get-tuple-element.314) | copy-start | bytes 7077892 | tf_op jit(solution)/shard_map/while
  103.7 4.8 %copy-start.5 = (bf16[394,768]{1,0:T(8,128)(2,1)S(1)}, bf16[394,768]{1,0:T(8,128)(2,1)}, u32[]{:S(2)}) copy-start(bf16[394,768]{1,0:T(8,128)(2,1)} %get-tuple-element.331) | copy-start | bytes 1815556 | tf_op jit(solution)/shard_map/while
  109.8 1.5 copy-start.2
  109.8 2.2 copy-start.4
  116.8 3.2 copy-start
  138.3 1.7 copy-start.7
  145.9 149.0 %copy-start.8 = (f32[24,768]{1,0:T(8,128)S(1)}, f32[24,768]{1,0:T(8,128)}, u32[]{:S(2)}) copy-start(f32[24,768]{1,0:T(8,128)} %param.16) | copy-start | bytes 221188
  145.9 149.0 %copy-start.9 = (f32[24,768]{1,0:T(8,128)S(1)}, f32[24,768]{1,0:T(8,128)}, u32[]{:S(2)}) copy-start(f32[24,768]{1,0:T(8,128)} %param.13) | copy-start | bytes 221188
  145.9 151.0 %all-to-all-start = ((f32[4,394,192]{1,2,0:T(8,128)}), f32[4,394,192]{1,2,0:T(8,128)S(1)}, u32[]{:S(2)}, u32[]{:S(2)}) async-start(f32[4,394,192]{1,2,0:T(8,128)} %copy.13), calls=%async_computation.1 | async-start | bytes 3145728 | tf_op jit(solution)/shard_map/all_to_all | solution.py:37
  292.6 43.5 %copy-start.12 = (f32[24,768]{1,0:T(8,128)S(1)}, f32[24,768]{1,0:T(8,128)}, u32[]{:S(2)}) copy-start(f32[24,768]{1,0:T(8,128)} %param.15) | copy-start | bytes 221188
  292.6 43.5 %copy-start.13 = (f32[24,768]{1,0:T(8,128)S(1)}, f32[24,768]{1,0:T(8,128)}, u32[]{:S(2)}) copy-start(f32[24,768]{1,0:T(8,128)} %param.12) | copy-start | bytes 221188
  295.6 41.3 %copy-start.10 = (f32[24,768]{1,0:T(8,128)}, f32[24,768]{1,0:T(8,128)S(1)}, u32[]{:S(2)}) copy-start(f32[24,768]{1,0:T(8,128)S(1)} %get-tuple-element.221) | copy-start | bytes 221188
  295.6 41.3 %copy-start.11 = (f32[24,768]{1,0:T(8,128)}, f32[24,768]{1,0:T(8,128)S(1)}, u32[]{:S(2)}) copy-start(f32[24,768]{1,0:T(8,128)S(1)} %get-tuple-element.222) | copy-start | bytes 221188
Sparse Core Ops, SparseCore 0:
  11.1 79.7 all-gather.2
  138.4 153.2 reduce-scatter.1
where the time goes:
time: 344 us
  waiting for transfers between devices  223 us (65%)
  blocking collectives  39.6 us (12%)
  local copies, waits for them, and re-layouts  32 us (9%)
  matrix products  18.2 us (5%)
  between operations  16.2 us (5%)
  other arithmetic  9.72 us (3%)
  starting transfers between devices  4.49 us (1%)
    reduce_scatter x1, waiting for transfers between devices, sum_together(): lax.psum_scatter(lines, axis, tiled=True).reshape(-1)  141 us
    all_gather x1, waiting for transfers between devices, sent_together(): filled = lax.all_gather(both, axis, axis=dim, tiled=True)  81.9 us
    psum x3, blocking collectives, one_axis_at_a_time(): value = lax.psum(value, axis)  37.4 us
    dot_general x4, matrix products, contract_rows(): lax.dot_general(left, right, (((0,), (0,)), ((), ())), preferred_element_...  11.4 us
    reshape x1, local copies, waits for them, and re-layouts, sum_together(): jnp.pad(lines, ((0, 0), (0, span * 128 - lines.shape[1]))).reshape(-1, 128)  9.96 us
    another operation x4, local copies, waits for them, and re-layouts, sum_together(): lines = jnp.concatenate([b.reshape(devices, -1) for b in tiles], axis=1)  9.89 us
  transfers between devices with their start and end apart: 3, of which 2 were waited for; matrix products, arithmetic and copies ran while one was open for 2% of the time, Pallas kernels for 0%

commit v1 on v0

--- a/solution.py
+++ b/solution.py
@@ -54,7 +54,7 @@
 
 def one_axis_at_a_time(value, axes):
     for axis in axes:
-        value = lax.psum(value, axis)
+        value = jnp.sum(lax.all_gather(value, axis), axis=0)
     return value
 
 

time: 344 us -> 348 us (1.012)
  local copies, waits for them, and re-layouts: 32 us -> 37.3 us
    psum x3 -> x0, blocking collectives: 37.4 us -> none  [one_axis_at_a_time(): value = lax.psum(value, axis)]
    unnamed x0 -> x3, blocking collectives: none -> 35.6 us
    unnamed x21 -> x36, local copies, waits for them, and re-layouts: 2.64 us -> 7.95 us
  transfers between devices with their start and end apart: 3 -> 3, of which waited for: 2 -> 2; matrix products, arithmetic and copies ran while one was open for 2% -> 3% of each run, Pallas kernels for 0% -> 0%
where the time goes in v1:
time: 348 us; the launch traced here: 347 us
  waiting for transfers between devices  222 us (64%)
  blocking collectives  37.8 us (11%)
  local copies, waits for them, and re-layouts  37.3 us (11%)
  matrix products  18.2 us (5%)
  between operations  16.3 us (5%)
  other arithmetic  11.5 us (3%)
  starting transfers between devices  4.5 us (1%)
    reduce_scatter x1, waiting for transfers between devices, sum_together(): lax.psum_scatter(lines, axis, tiled=True).reshape(-1)  140 us
    all_gather x1, waiting for transfers between devices, sent_together(): filled = lax.all_gather(both, axis, axis=dim, tiled=True)  81.9 us
    unnamed x3, blocking collectives  35.6 us
    dot_general x4, matrix products, contract_rows(): lax.dot_general(left, right, (((0,), (0,)), ((), ())), preferred_element_...  11.4 us
    reshape x1, local copies, waits for them, and re-layouts, sum_together(): jnp.pad(lines, ((0, 0), (0, span * 128 - lines.shape[1]))).reshape(-1, 128)  9.95 us
    another operation x4, local copies, waits for them, and re-layouts, sum_together(): lines = jnp.concatenate([b.reshape(devices, -1) for b in tiles], axis=1)  9.9 us
    unnamed x36, local copies, waits for them, and re-layouts  7.95 us
  transfers between devices with their start and end apart: 3, of which 2 were waited for; matrix products, arithmetic and copies ran while one was open for 3% of the time, Pallas kernels for 0%

profile of v1, /device:TPU:2, one launch (start us, length us, event | category | flops | bytes accessed | tf_op | source)
XLA Modules:
  0.0 347.4 jit_solution(8664696452332603258)
XLA Ops:
  9.1 81.9 %all-gather.3.cloned.1.call-done = bf16[768,1536]{1,0:T(8,128)(2,1)} async-done(((bf16[24,1536]{1,0:T(8,128)(2,1)}), bf16[768,1536]{1,0:T(8,128)(2,1)}) %all-gather.3.cloned.1.call-update) | async-done | bytes 2359312 | tf_op jit(solution)/shard_map/all_gather | solution.py:25
  90.9 3.1 multiply_convert_fusion
  94.1 2.0 fusion.9
  96.1 15.9 %while.20 = (s32[]{:T(128)}, f32[768,768]{1,0:T(8,128)}, f32[768,768]{1,0:T(8,128)}, f32[768,768]{1,0:T(8,128)}, f32[768,768]{1,0:T(8,128)S(1)}, /*index=5*/bf16...) while((s32[]{:T(128)}, f32[768,768]{1,0:T(8,128)}, ...), condition=%wide.region_1.0_spmd.clone, body=%wide.region_0.0_spmd.clone.sunk | while | flops 470679552 | bytes 60276036 | solution.py:116
  96.1 4.0 %select_add_fusion.7 = (f32[768,768]{1,0:T(8,128)S(1)}, f32[768,768]{1,0:T(8,128)}) fusion(f32[768,768]{1,0:T(8,128)S(1)} %get-tuple-element.317, pred[]{:T(512)S(6)} %compare.3, f32[768,768]{1,0:T(8,128)} %get-tuple-element.316, bf16[394,768]{1,0:T(8,128)(2,1)} %get-tuple-element.334, s32[]{:T(128)S(6)} %select_n.12, ...), kind=kOutput, calls=%fused_computation.clone.1 | convolution fusion | flops 235339776 | bytes 10053120 | tf_op jit(solution)/shard_map/while/body/eval_jaxpr/dot_general | solution.py:73
  101.5 1.4 copy-done.2
  103.7 4.7 %select_add_fusion.7 = (f32[768,768]{1,0:T(8,128)S(1)}, f32[768,768]{1,0:T(8,128)}) fusion(f32[768,768]{1,0:T(8,128)S(1)} %get-tuple-element.317, pred[]{:T(512)S(6)} %compare.3, f32[768,768]{1,0:T(8,128)} %get-tuple-element.316, bf16[394,768]{1,0:T(8,128)(2,1)} %get-tuple-element.334, s32[]{:T(128)S(6)} %select_n.12, ...), kind=kOutput, calls=%fused_computation.clone.1 | convolution fusion | flops 235339776 | bytes 10053120 | tf_op jit(solution)/shard_map/while/body/eval_jaxpr/dot_general | solution.py:73
  109.8 1.4 copy-done.2
  112.0 1.8 reshape_reshape.15
  113.8 3.0 reshape_reshape.12
  116.8 3.2 reshape_reshape.13
  120.1 1.8 reshape_reshape.14
  121.9 6.4 %pad_maximum_fusion = f32[64,36864]{1,0:T(8,128)} fusion(f32[64,9216]{1,0:T(8,128)} %reshape_reshape.15, f32[64,9216]{1,0:T(8,128)} %reshape_reshape.14, f32[64,9216]{1,0:T(8,128)} %reshape_reshape.13, f32[64,9216]{1,0:T(8,128)} %reshape_reshape.12), kind=kLoop, calls=%fused_computation.12 | loop fusion | flops 7077888 | bytes 18874368 | tf_op jit(solution)/shard_map/concatenate | solution.py:44
  128.3 9.9 %reshape.45 = f32[18432,128]{1,0:T(8,128)} reshape(f32[64,36864]{1,0:T(8,128)} %pad_maximum_fusion) | data formatting | bytes 18874368 | tf_op jit(solution)/shard_map/reshape | solution.py:46
  138.3 1.6 copy-done.7
  139.9 1.7 fusion.15
  141.6 2.4 reshape.50
  144.0 1.8 copy.13
  145.9 4.4 %all-to-all-start = ((f32[4,394,192]{1,2,0:T(8,128)}), f32[4,394,192]{1,2,0:T(8,128)S(1)}, u32[]{:S(2)}, u32[]{:S(2)}) async-start(f32[4,394,192]{1,2,0:T(8,128)} %copy.13), calls=%async_computation.1 | async-start | bytes 3145728 | tf_op jit(solution)/shard_map/all_to_all | solution.py:37
  152.1 139.8 %reduce-scatter.2.cloned.1.call-done = f32[288,128]{1,0:T(8,128)} async-done(((f32[18432,128]{1,0:T(8,128)}), f32[288,128]{1,0:T(8,128)}) %reduce-scatter.2.cloned.1.call-update) | async-done | bytes 147472 | tf_op jit(solution)/shard_map/reduce_scatter | solution.py:47
  292.8 2.2 all-gather
  298.0 15.6 %all-reduce = f32[8]{0:T(128)S(1)} all-reduce(f32[8]{0:T(128)S(1)} %dynamic-update-slice), channel_id=1, replica_groups=mesh['dp_0'=8,'dp_1'=4,'mp'=4,'mc'=2] {'dp_0'}, use_global_device_ids=true, to_apply=%add | all-reduce | flops 8 | bytes 64
  315.7 9.5 %all-reduce.1 = f32[4]{0:T(128)S(1)} all-reduce(f32[4]{0:T(128)S(1)} %dynamic-update-slice.1), channel_id=1, replica_groups=mesh['dp_0'=8,'dp_1'=4,'mp'=4,'mc'=2] {'dp_1'}, use_global_device_ids=true, to_apply=%add.1 | all-reduce | flops 4 | bytes 32
  328.0 10.5 %all-reduce.2 = f32[4]{0:T(128)S(1)} all-reduce(f32[4]{0:T(128)S(1)} %dynamic-update-slice.2), channel_id=1, replica_groups=mesh['dp_0'=8,'dp_1'=4,'mp'=4,'mc'=2] {'mp'}, use_global_device_ids=true, to_apply=%add.2 | all-reduce | flops 4 | bytes 32
  (78 shorter events, 16.6 us)
Async XLA Ops:
  7.2 83.8 %all-gather.3.cloned.1.call-start = ((), (), s32[]{:S(2)}) async-start(), calls=%async_computation.2 | async-start | bytes 2433024 | tf_op jit(solution)/shard_map/all_gather | solution.py:25
  9.0 282.9 %reduce-scatter.2.cloned.1.call-start = ((), (), s32[]{:S(2)}) async-start(), calls=%async_computation.3 | async-start | bytes 9584640 | tf_op jit(solution)/shard_map/reduce_scatter | solution.py:47
  90.9 3.1 copy-start.6
  96.1 4.0 %copy-start.1 = (f32[768,768]{1,0:T(8,128)S(1)}, f32[768,768]{1,0:T(8,128)}, u32[]{:S(2)}) copy-start(f32[768,768]{1,0:T(8,128)} %get-tuple-element.315) | copy-start | bytes 7077892 | tf_op jit(solution)/shard_map/while
  96.1 4.0 %copy-start.3 = (f32[768,768]{1,0:T(8,128)S(1)}, f32[768,768]{1,0:T(8,128)}, u32[]{:S(2)}) copy-start(f32[768,768]{1,0:T(8,128)} %get-tuple-element.314) | copy-start | bytes 7077892 | tf_op jit(solution)/shard_map/while
  96.1 4.0 %copy-start.5 = (bf16[394,768]{1,0:T(8,128)(2,1)S(1)}, bf16[394,768]{1,0:T(8,128)(2,1)}, u32[]{:S(2)}) copy-start(bf16[394,768]{1,0:T(8,128)(2,1)} %get-tuple-element.331) | copy-start | bytes 1815556 | tf_op jit(solution)/shard_map/while
  101.4 1.5 copy-start.2
  101.5 2.2 copy-start.4
  103.7 4.7 %copy-start.1 = (f32[768,768]{1,0:T(8,128)S(1)}, f32[768,768]{1,0:T(8,128)}, u32[]{:S(2)}) copy-start(f32[768,768]{1,0:T(8,128)} %get-tuple-element.315) | copy-start | bytes 7077892 | tf_op jit(solution)/shard_map/while
  103.7 4.7 %copy-start.3 = (f32[768,768]{1,0:T(8,128)S(1)}, f32[768,768]{1,0:T(8,128)}, u32[]{:S(2)}) copy-start(f32[768,768]{1,0:T(8,128)} %get-tuple-element.314) | copy-start | bytes 7077892 | tf_op jit(solution)/shard_map/while
  103.7 4.7 %copy-start.5 = (bf16[394,768]{1,0:T(8,128)(2,1)S(1)}, bf16[394,768]{1,0:T(8,128)(2,1)}, u32[]{:S(2)}) copy-start(bf16[394,768]{1,0:T(8,128)(2,1)} %get-tuple-element.331) | copy-start | bytes 1815556 | tf_op jit(solution)/shard_map/while
  109.8 2.2 copy-start.4
  116.8 3.2 copy-start
  138.3 1.7 copy-start.7
  145.8 4.4 %copy-start.16 = (u32[256]{0:T(256)S(1)}, u32[256]{0:T(256)}, u32[]{:S(2)}) copy-start(u32[256]{0:T(256)} %constant.88) | copy-start | bytes 3076
  145.8 5.0 %copy-start.15 = (u32[256]{0:T(256)S(1)}, u32[256]{0:T(256)}, u32[]{:S(2)}) copy-start(u32[256]{0:T(256)} %constant.83) | copy-start | bytes 3076
  145.8 5.7 %copy-start.14 = (u32[256]{0:T(256)S(1)}, u32[256]{0:T(256)}, u32[]{:S(2)}) copy-start(u32[256]{0:T(256)} %constant.78) | copy-start | bytes 3076
  145.8 149.3 %copy-start.8 = (f32[24,768]{1,0:T(8,128)S(1)}, f32[24,768]{1,0:T(8,128)}, u32[]{:S(2)}) copy-start(f32[24,768]{1,0:T(8,128)} %param.16) | copy-start | bytes 221188
  145.8 149.3 %copy-start.9 = (f32[24,768]{1,0:T(8,128)S(1)}, f32[24,768]{1,0:T(8,128)}, u32[]{:S(2)}) copy-start(f32[24,768]{1,0:T(8,128)} %param.13) | copy-start | bytes 221188
  145.9 152.0 %all-to-all-start = ((f32[4,394,192]{1,2,0:T(8,128)}), f32[4,394,192]{1,2,0:T(8,128)S(1)}, u32[]{:S(2)}, u32[]{:S(2)}) async-start(f32[4,394,192]{1,2,0:T(8,128)} %copy.13), calls=%async_computation.1 | async-start | bytes 3145728 | tf_op jit(solution)/shard_map/all_to_all | solution.py:37
  292.8 47.0 %copy-start.12 = (f32[24,768]{1,0:T(8,128)S(1)}, f32[24,768]{1,0:T(8,128)}, u32[]{:S(2)}) copy-start(f32[24,768]{1,0:T(8,128)} %param.15) | copy-start | bytes 221188
  292.8 47.0 %copy-start.13 = (f32[24,768]{1,0:T(8,128)S(1)}, f32[24,768]{1,0:T(8,128)}, u32[]{:S(2)}) copy-start(f32[24,768]{1,0:T(8,128)} %param.12) | copy-start | bytes 221188
  295.8 44.8 %copy-start.10 = (f32[24,768]{1,0:T(8,128)}, f32[24,768]{1,0:T(8,128)S(1)}, u32[]{:S(2)}) copy-start(f32[24,768]{1,0:T(8,128)S(1)} %get-tuple-element.221) | copy-start | bytes 221188
  295.8 44.8 %copy-start.11 = (f32[24,768]{1,0:T(8,128)}, f32[24,768]{1,0:T(8,128)S(1)}, u32[]{:S(2)}) copy-start(f32[24,768]{1,0:T(8,128)S(1)} %get-tuple-element.222) | copy-start | bytes 221188
  (1 other events, 1.5 us)
Sparse Core Ops, SparseCore 0:
  11.1 79.7 all-gather.2
  138.4 153.4 reduce-scatter.1
